TPU v7x, 32 devices: a whole 2x2x4 slice. The times are simulated.
32 devices in a mesh: context: 8 (over z, y), tensor: 4 (over x, core).
Axes of the slice: x: 2, y: 2, z: 4, core: 2. Of those that a mesh axis runs over, the one named last changes fastest.
Arguments:
- hidden: bfloat16 [256, 4096], P('context', 'tensor'), may hold values from -270 to 270
- weight: bfloat16 [4096, 128256], P(None, ('context', 'tensor')), may hold values from -0.25 to 0.25
- targets: int32 [256], P('context'), may hold values from 0 to 128255
- mask: int32 [256], P('context'), may hold values 0 or 1
- loss_scale: float32 [], replicated, may hold values from 2048 to 32768
Outputs:
- loss: float32 [], replicated
- grad_hidden: bfloat16 [256, 4096], P('context', 'tensor')
- grad_weight: bfloat16 [4096, 128256], P(None, ('context', 'tensor'))
All inputs are finite; a program needn't handle non-finite values. No bound on the sum of `mask` on one device may be relied on, other than what follows from the above.
Results may differ from a plain program's by a relative error of at most 0.0052.
Values may be sent and summed in bfloat16 or wider, within the bound.
No kernel may reach another device: no remote copies, remote signals or barrier semaphores. Data moves between devices by JAX's collectives and lax.ppermute only.
A program may use at most 192 MiB of HBM per device.

v0:
```python
import jax
import jax.numpy as jnp
from jax import lax
from jax.sharding import PartitionSpec as P

clip_limit = 1.0


def joined(value, axis, join):
    pieces = jax.tree.map(lambda part: lax.all_gather(part, axis), value)
    head = jax.tree.map(lambda part: part[0], pieces)
    tail = jax.tree.map(lambda part: part[1:], pieces)
    total, _ = lax.scan(lambda total, piece: (join(total, piece), None), head, tail)
    return total


def combine(first, second):
    top = jnp.maximum(first[0], second[0])
    total = first[1] * jnp.exp(first[0] - top) + second[1] * jnp.exp(second[0] - top)
    return (top, total, first[2] + second[2])


def shards(hidden, weight, targets, mask, loss_scale):
    rows = lax.all_gather(hidden, "tensor", axis=1, tiled=True)
    all_rows, all_targets, all_mask = (
        lax.all_gather(rows, "context", axis=0, tiled=True),
        lax.all_gather(targets, "context", axis=0, tiled=True),
        lax.all_gather(mask, "context", axis=0, tiled=True),
    )
    vocab_dev = weight.shape[1]
    offset = lax.axis_index(("context", "tensor")) * vocab_dev
    logits = jnp.dot(all_rows, weight, preferred_element_type=jnp.float32)
    columns = offset + lax.broadcasted_iota(jnp.int32, (1, vocab_dev), 1)
    onehot = (columns == all_targets[:, None]).astype(jnp.float32)
    local_target = jnp.sum(logits * onehot, axis=1)
    local_max = jnp.max(logits, axis=1)
    local_sum = jnp.sum(jnp.exp(logits - local_max[:, None]), axis=1)
    partial_stats = joined((local_max, local_sum, local_target), "tensor", combine)
    row_max, sum_exp, target_logit = joined(partial_stats, "context", combine)
    shifted = jnp.exp(logits - row_max[:, None])
    maskf = all_mask.astype(jnp.float32)
    denom = jnp.maximum(jnp.sum(maskf), jnp.float32(1.0))
    token_loss = jnp.log(sum_exp) + row_max - target_logit
    loss = jnp.sum(maskf * token_loss) / denom
    factor = loss_scale * maskf / denom
    grad_logits = (factor[:, None] * (shifted / sum_exp[:, None] - onehot)).astype(jnp.bfloat16)
    raw_grad = lax.dot_general(
        all_rows, grad_logits, (((0,), (0,)), ((), ())), preferred_element_type=jnp.float32
    )
    squares = lax.psum(jnp.sum(raw_grad * raw_grad), ("context", "tensor"))
    full_term = lax.dot_general(
        grad_logits, weight, (((1,), (1,)), ((), ())), preferred_element_type=jnp.float32
    )
    feature_part = lax.psum_scatter(full_term, "tensor", scatter_dimension=1, tiled=True)
    summed = lax.psum_scatter(feature_part, "context", scatter_dimension=0, tiled=True)
    grad_hidden = summed.astype(jnp.bfloat16)
    grad_norm = jnp.sqrt(squares) / loss_scale
    grad_weight = (raw_grad * (clip_limit / jnp.maximum(grad_norm, clip_limit))).astype(
        jnp.bfloat16
    )
    return (loss, grad_hidden, grad_weight)


def solution(mesh):
    placed = (
        P("context", "tensor"),
        P(None, ("context", "tensor")),
        P("context"),
        P("context"),
        P(),
    )
    return jax.shard_map(
        shards,
        mesh=mesh,
        in_specs=placed,
        out_specs=(P(), P("context", "tensor"), P(None, ("context", "tensor"))),
        check_vma=False,
    )
```

profile of v0, /device:TPU:0, one launch (start us, length us, event | category | flops | bytes accessed | tf_op | source)
XLA Modules:
  0.0 315.4 jit_solution(7631644702573730922)
XLA Ops:
  7.2 0.0 all-gather.14.cloned.1.call-start
  7.2 8.8 %all_gather.49 = bf16[32,4096]{1,0:T(8,128)(2,1)} all-gather(bf16[32,1024]{1,0:T(8,128)(2,1)} %param.9), channel_id=1, replica_groups=mesh['context'=8,'tensor'=4] {'tensor'}, dimensions={1}, use_global_device_ids=true | all-gather | bytes 327680 | tf_op jit(solution)/shard_map/all_gather | solution.py:24
  16.1 0.0 all-gather.14.cloned.1.call-update
  16.1 0.0 reduce-scatter.3.cloned.1.call-start
  16.8 1.2 dynamic-slice
  18.7 0.9 dynamic-update-slice
  19.6 0.8 dynamic-update-slice.1
  20.4 11.7 %all-reduce.2 = (s32[256]{0:T(256)S(1)}, s32[256]{0:T(256)S(1)}) all-reduce(s32[256]{0:T(256)S(1)} %dynamic-update-slice, s32[256]{0:T(256)S(1)} %dynamic-update-slice.1), channel_id=1, replica_groups=mesh['context'=8,'tensor'=4] {'context'}, use_global_device_ids=true, to_apply=%add | all-reduce | flops 512 | bytes 4096
  32.1 33.6 %all-gather.14.cloned.1.call-done = bf16[256,4096]{1,0:T(8,128)(2,1)} async-done(((bf16[32,4096]{1,0:T(8,128)(2,1)}), bf16[256,4096]{1,0:T(8,128)(2,1)}) %all-gather.14.cloned.1.call-update) | async-done | bytes 2097168 | tf_op jit(solution)/shard_map/all_gather | solution.py:26
  65.6 14.7 %fusion.9 = (f32[256]{0:T(256)S(1)}, f32[256,4008]{0,1:T(8,128)S(1)}) fusion(bf16[256,4096]{1,0:T(8,128)(2,1)} %all-gather.14.cloned.1.call-done, bf16[4096,4008]{0,1:T(8,128)(2,1)} %param.10), kind=kOutput, calls=%fused_computation.30 | convolution fusion | flops 8406411264 | bytes 39035904 | tf_op jit(solution)/shard_map/dot_general | solution.py:32
  80.4 0.0 copy-start
  80.4 2.0 copy-done
  82.4 1.8 fusion.1
  84.2 5.1 %all-gather.7 = f32[4,1,256]{2,1,0:T(1,128)S(1)} all-gather(f32[1,1,256]{2,1,0:T(1,128)S(1)} %bitcast.78), channel_id=3, replica_groups=mesh['context'=8,'tensor'=4] {'tensor'}, dimensions={0}, use_global_device_ids=true | all-gather | bytes 5120 | tf_op jit(solution)/shard_map/all_gather | solution.py:10
  89.3 5.1 %all-gather.8 = f32[4,1,256]{2,1,0:T(1,128)S(1)} all-gather(f32[1,1,256]{2,1,0:T(1,128)S(1)} %bitcast.77), channel_id=4, replica_groups=mesh['context'=8,'tensor'=4] {'tensor'}, dimensions={0}, use_global_device_ids=true | all-gather | bytes 5120 | tf_op jit(solution)/shard_map/all_gather | solution.py:10
  94.3 5.1 %all-gather.6 = f32[4,1,256]{2,1,0:T(1,128)S(1)} all-gather(f32[1,1,256]{2,1,0:T(1,128)S(1)} %bitcast.76), channel_id=2, replica_groups=mesh['context'=8,'tensor'=4] {'tensor'}, dimensions={0}, use_global_device_ids=true | all-gather | bytes 5120 | tf_op jit(solution)/shard_map/all_gather | solution.py:10
  99.4 0.2 while.28
  99.6 18.1 %all-gather.9 = f32[8,1,256]{2,1,0:T(1,128)S(1)} all-gather(f32[1,1,256]{2,1,0:T(1,128)S(1)} %bitcast.69), channel_id=5, replica_groups=mesh['context'=8,'tensor'=4] {'context'}, dimensions={0}, use_global_device_ids=true | all-gather | bytes 9216 | tf_op jit(solution)/shard_map/all_gather | solution.py:10
  117.8 16.5 %all-gather.11 = f32[8,1,256]{2,1,0:T(1,128)S(1)} all-gather(f32[1,1,256]{2,1,0:T(1,128)S(1)} %bitcast.65), channel_id=7, replica_groups=mesh['context'=8,'tensor'=4] {'context'}, dimensions={0}, use_global_device_ids=true | all-gather | bytes 9216 | tf_op jit(solution)/shard_map/all_gather | solution.py:10
  134.2 18.1 %all-gather.10 = f32[8,1,256]{2,1,0:T(1,128)S(1)} all-gather(f32[1,1,256]{2,1,0:T(1,128)S(1)} %bitcast.67), channel_id=6, replica_groups=mesh['context'=8,'tensor'=4] {'context'}, dimensions={0}, use_global_device_ids=true | all-gather | bytes 9216 | tf_op jit(solution)/shard_map/all_gather | solution.py:10
  152.4 0.6 while.29
  152.9 0.6 convert_reduce_fusion
  154.2 19.0 %fusion.7 = f32[256,4096]{1,0:T(8,128)} fusion(bf16[4096,4008]{0,1:T(8,128)(2,1)} %param.10, f32[256,4008]{0,1:T(8,128)} %copy-done, f32[256]{0:T(256)S(1)} %get-tuple-element.84, f32[256]{0:T(256)S(1)} %get-tuple-element.85, f32[256]{0:T(256)S(1)} %multiply_divide_fusion, s32[256]{0:T(256)S(1)} %get-tuple-element.120, s32[4008]{0:T(1024)S(1)} %iota_add_fusion), kind=kOutput, calls=%fused_computation.29 | convolution fusion | flops 8412567552 | bytes 41152160 | tf_op jit(solution)/shard_map/dot_general | solution.py:51
  173.2 0.0 copy-start.1
  173.2 0.0 reduce-scatter.3.cloned.1.call-update
  173.2 0.2 reduce-scatter.5.cloned.1.call-start
  173.5 1.3 copy-done.1
  174.8 27.5 %multiply_reduce_fusion = (f32[]{:T(128)}, f32[4008,4096]{1,0:T(8,128)}) fusion(bf16[256,4096]{1,0:T(8,128)(2,1)S(1)} %copy-done.1, f32[256,4008]{0,1:T(8,128)} %copy-done, f32[256]{0:T(256)S(1)} %get-tuple-element.84, f32[256]{0:T(256)S(1)} %get-tuple-element.85, f32[256]{0:T(256)S(1)} %multiply_divide_fusion, s32[256]{0:T(256)S(1)} %get-tuple-element.120, ...), kind=kOutput, calls=%fused_computation.9 | convolution fusion | flops 8445401088 | bytes 71888544 | tf_op jit(solution)/shard_map/dot_general | solution.py:47
  202.3 37.6 %psum.7 = f32[]{:T(128)} all-reduce(f32[]{:T(128)} %get-tuple-element.131), channel_id=1, replica_groups=mesh['context'=8,'tensor'=4] {'context','tensor'}, use_global_device_ids=true, to_apply=%region_12.13 | all-reduce | flops 1 | bytes 8 | tf_op jit(solution)/shard_map/psum | solution.py:50
  240.7 0.0 reduce-scatter.3.cloned.1.call-done
  240.7 0.0 reduce-scatter.5.cloned.1.call-update
  240.8 32.4 %fusion = bf16[4096,4008]{0,1:T(8,128)(2,1)} fusion(f32[4008,4096]{1,0:T(8,128)} %get-tuple-element.132, f32[]{:T(128)S(6)} %div.29), kind=kLoop, calls=%fused_computation.10 | loop fusion | flops 32833536 | bytes 98500608 | tf_op jit(solution)/shard_map/convert_element_type | solution.py:58
  273.9 32.3 %reduce-scatter.5.cloned.1.call-done = f32[32,1024]{1,0:T(8,128)} async-done(((f32[256,1024]{1,0:T(8,128)}), f32[32,1024]{1,0:T(8,128)}) %reduce-scatter.5.cloned.1.call-update) | async-done | bytes 131088 | tf_op jit(solution)/shard_map/reduce_scatter | solution.py:55
  306.2 1.5 convert_element_type.21
  (62 shorter events, 0.5 us)
Async XLA Ops:
  7.2 58.5 %all-gather.14.cloned.1.call-start = ((), (), s32[]{:S(2)}) async-start(), calls=%async_computation.2 | async-start | bytes 2359296 | tf_op jit(solution)/shard_map/all_gather | solution.py:26
  16.1 224.7 %reduce-scatter.3.cloned.1.call-start = ((), (), s32[]{:S(2)}) async-start(), calls=%async_computation.3 | async-start | bytes 5242880 | tf_op jit(solution)/shard_map/reduce_scatter | solution.py:54
  80.4 2.0 copy-start
  173.2 1.6 copy-start.1
  173.2 133.0 %reduce-scatter.5.cloned.1.call-start = ((), (), s32[]{:S(2)}) async-start(), calls=%async_computation.4 | async-start | bytes 1179648 | tf_op jit(solution)/shard_map/reduce_scatter | solution.py:55
Sparse Core Ops, SparseCore 0:
  16.2 49.3 all-gather.13
  173.4 42.1 reduce-scatter.2
  240.9 65.2 reduce-scatter.4
where the time goes:
time: 316 us; the launch traced here: 315 us
  blocking collectives  126 us (40%)
  waiting for transfers between devices  66 us (21%)
  matrix products  61.3 us (19%)
  other arithmetic  36.7 us (12%)
  between operations  18.4 us (6%)
  local copies, waits for them, and re-layouts  6.46 us (2%)
    all_gather x6, blocking collectives, joined(): pieces = jax.tree.map(lambda part: lax.all_gather(part, axis), value)  67.9 us
    psum x1, blocking collectives, shards(): squares = lax.psum(jnp.sum(raw_grad * raw_grad), ('context', 'tensor'))  37.6 us
    all_gather x1, waiting for transfers between devices, shards(): lax.all_gather(rows, 'context', axis=0, tiled=True)  33.6 us
    convert_element_type x1, other arithmetic, shards(): (raw_grad * (clip_limit / jnp.maximum(grad_norm, clip_limit))).astype(jnp...  32.4 us
    reduce_scatter x1, waiting for transfers between devices, shards(): lax.psum_scatter(feature_part, 'context', scatter_dimension=0, tiled=True)  32.3 us
    dot_general x1, matrix products, shards(): lax.dot_general(all_rows, grad_logits, (((0,), (0,)), ((), ())), preferre...  27.5 us
    dot_general x1, matrix products, shards(): lax.dot_general(grad_logits, weight, (((1,), (1,)), ((), ())), preferred_...  19 us
    dot_general x1, matrix products, shards(): logits = jnp.dot(all_rows, weight, preferred_element_type=jnp.float32)  14.7 us
  transfers between devices with their start and end apart: 3, of which 2 were waited for; matrix products, arithmetic and copies ran while one was open for 20% of the time, Pallas kernels for 0%

commit v1 on v0

v1 whole, which is shorter than its diff:
```python
import functools

import jax
import jax.numpy as jnp
from jax import lax
from jax.experimental import pallas as pl
from jax.experimental.pallas import tpu as pltpu
from jax.sharding import PartitionSpec as P

clip_limit = 1.0
both = ("context", "tensor")
lowest = -1e30
f32 = jnp.float32
bf16 = jnp.bfloat16


def cost(flops, moved):
    return pl.CostEstimate(flops=int(flops), bytes_accessed=int(moved), transcendentals=0)


def divisor(size, most):
    best = size
    while best > most and best % 2 == 0:
        best //= 2
    return best


def hop(value, ctx, ten, dz, dy, dx, dc):
    pairs = []
    for source in range(ctx * ten):
        place, part = divmod(source, ten)
        other = ((place // 2 ^ dz) * 2 + (place % 2 ^ dy)) * ten
        pairs.append((source, other + (part // 2 ^ dx) * 2 + (part % 2 ^ dc)))
    return lax.ppermute(value, both, pairs)


def gathered(hidden, ctx, ten):
    levels = ctx // 2
    half = levels // 2
    go = functools.partial(hop, ctx=ctx, ten=ten)
    mine = jnp.stack(
        [hidden] + [go(hidden, dz=d, dy=0, dx=0, dc=0) for d in range(1, levels)]
    )
    across = go(mine, dz=0, dy=0, dx=1, dc=0)
    beside = go(mine, dz=0, dy=1, dx=0, dc=0)
    low = go(beside[:half], dz=0, dy=0, dx=1, dc=0)
    high = go(across[half:], dz=0, dy=1, dx=0, dc=0)
    found = [
        (mine, 0, 0, 0),
        (across, 0, 1, 0),
        (beside, 0, 0, 1),
        (low, 0, 1, 1),
        (high, half, 1, 1),
    ]
    pieces, places = [], []
    for flip in (0, 1):
        for block, first, dx, dy in found:
            pieces.append(go(block, dz=0, dy=0, dx=0, dc=1) if flip else block)
            places.append((tuple(range(first, first + block.shape[0])), dx, dy, flip))
    return pieces, tuple(places)


def logits_kernel(places, vocab, steps, at_ref, own_ref, *refs):
    pieces = refs[: len(places)]
    weight_ref, logits_ref, note_ref, hidden_ref, gram_ref, top_ref, sum_ref, sems = refs[
        len(places) :
    ]
    step = pl.program_id(0)
    z, y, x, c = (at_ref[k] for k in range(4))

    @pl.when(step == 0)
    def _():
        copies = []
        for piece, (levels, dx, dy, dc) in zip(pieces, places):
            _, rows, width = piece.shape
            for k, dz in enumerate(levels):
                row = pl.multiple_of(((z ^ dz) * 2 + (y ^ dy)) * rows, rows)
                column = pl.multiple_of(((x ^ dx) * 2 + (c ^ dc)) * width, width)
                copies.append(
                    pltpu.make_async_copy(
                        piece.at[k],
                        hidden_ref.at[pl.ds(row, rows), pl.ds(column, width)],
                        sems.at[len(copies)],
                    )
                )
        for copy in copies:
            copy.start()
        top_ref[...] = jnp.full_like(top_ref, lowest)
        sum_ref[...] = jnp.zeros_like(sum_ref)
        for copy in copies:
            copy.wait()
        gram_ref[...] = lax.dot_general(
            hidden_ref[...],
            hidden_ref[...],
            (((1,), (1,)), ((), ())),
            preferred_element_type=f32,
        )

    logits = lax.dot_general(
        weight_ref[...],
        hidden_ref[...],
        (((1,), (1,)), ((), ())),
        preferred_element_type=f32,
    )
    block = logits.shape[0]
    entries = step * block + lax.broadcasted_iota(jnp.int32, logits.shape, 0)
    logits = jnp.where(entries < vocab, logits, lowest)
    logits_ref[...] = logits
    old = top_ref[:1]
    top = jnp.maximum(old, jnp.max(logits, axis=0, keepdims=True))
    shifted = jnp.sum(jnp.exp(logits - top), axis=0, keepdims=True)
    sum_ref[:1] = sum_ref[:1] * jnp.exp(old - top) + shifted
    top_ref[:1] = top

    @pl.when(step == steps - 1)
    def _():
        rows = jnp.concatenate([top_ref[:1], sum_ref[:1], own_ref[2:]], axis=0)
        for device in range(note_ref.shape[0]):
            note_ref[device] = rows


def gradient_kernel(
    vocab, block, at_ref, notes_ref, scale_ref, logits_ref, gram_ref, weight_ref,
    part_ref, grad_ref, turned_ref, sums_ref,
):
    @pl.when(pl.program_id(0) == 0)
    def _():
        offset = at_ref[4]
        notes = notes_ref[...]
        tops = notes[:, 0, :]
        top = jnp.max(tops, axis=0, keepdims=True)
        total = jnp.sum(notes[:, 1, :] * jnp.exp(tops - top), axis=0, keepdims=True)
        target = jnp.sum(notes[:, 2, :], axis=0, keepdims=True)
        mask = jnp.sum(notes[:, 3, :], axis=0, keepdims=True)
        denom = jnp.maximum(jnp.sum(mask, axis=1, keepdims=True), 1.0)
        factor = scale_ref[0, 0] * mask / denom
        rate = factor / total
        known = jnp.sum(mask * (jnp.log(total) + top), axis=1, keepdims=True)
        spot = target.astype(jnp.int32) - offset
        spot = jnp.where(spot < vocab, spot, -1)
        gram = jnp.zeros(gram_ref.shape, f32)
        hit = jnp.zeros(spot.shape, f32)
        for start in range(0, logits_ref.shape[0], block):
            logits = logits_ref[start : start + block]
            entries = start + lax.broadcasted_iota(jnp.int32, logits.shape, 0)
            chosen = entries == spot
            hit += jnp.sum(jnp.where(chosen, logits, 0.0), axis=0, keepdims=True)
            grad = rate * jnp.exp(logits - top) - jnp.where(chosen, factor, 0.0)
            grad = grad.astype(bf16)
            grad_ref[start : start + block] = grad
            turned = jnp.transpose(grad)
            turned_ref[:, start : start + block] = turned
            gram += jnp.dot(turned, grad, preferred_element_type=f32)
        squares = jnp.sum(
            jnp.sum(gram * gram_ref[...], axis=1, keepdims=True), axis=0, keepdims=True
        )
        hits = jnp.sum(mask * hit, axis=1, keepdims=True)
        lanes = lax.broadcasted_iota(jnp.int32, sums_ref.shape, 1)
        sums_ref[...] = jnp.where(
            lanes == 0,
            squares,
            jnp.where(lanes == 1, hits, jnp.where(lanes == 2, known, denom)),
        )

    part_ref[0] = jnp.dot(
        turned_ref[:, :vocab], weight_ref[...], preferred_element_type=f32
    ).astype(part_ref.dtype)


def product_kernel(vocab, at_ref, turned_ref, weight_ref, part_ref):
    part_ref[0] = jnp.dot(
        turned_ref[:, :vocab], weight_ref[...], preferred_element_type=f32
    ).astype(part_ref.dtype)


def outer_kernel(width, rate_ref, hidden_ref, grad_ref, out_ref):
    rate = rate_ref[0, 0]
    for start in range(0, out_ref.shape[1], width):
        raw = jnp.dot(
            grad_ref[...], hidden_ref[:, start : start + width], preferred_element_type=f32
        )
        out_ref[:, start : start + width] = (raw * rate).astype(bf16)


def encoded(values):
    first = lax.reduce_precision(values, 8, 7)
    second = lax.reduce_precision(values - first, 8, 7)
    third = lax.reduce_precision(values - first - second, 8, 7)
    return jnp.concatenate([first, second, third])


def decoded(row, count):
    terms = row[: 3 * count].astype(f32)
    return terms[:count] + terms[count : 2 * count] + terms[2 * count :]


def packed(block, values, width):
    flat = block.astype(bf16).reshape(-1, width)
    row = jnp.pad(encoded(values), (0, width - 3 * values.shape[0])).astype(bf16)
    return jnp.concatenate([flat, jnp.broadcast_to(row[None], (8, width))])


def shards(ctx, ten, hidden, weight, targets, mask, loss_scale):
    rows, width = hidden.shape
    model, vocab = weight.shape
    table = weight.T
    tokens = rows * ctx
    devices = ctx * ten
    levels = ctx // 2
    half = levels // 2
    place, part = lax.axis_index("context"), lax.axis_index("tensor")
    z, y, x, c = place // 2, place % 2, part // 2, part % 2
    offset = (place * ten + part) * vocab
    at = jnp.stack([z, y, x, c, offset]).astype(jnp.int32)
    go = functools.partial(hop, ctx=ctx, ten=ten)

    own = jnp.stack([targets, mask]).astype(f32) * (part == 0).astype(f32)
    own = lax.dynamic_update_slice(
        jnp.zeros((8, tokens), f32), own, (jnp.int32(2), (place * rows).astype(jnp.int32))
    )
    pieces, places = gathered(hidden, ctx, ten)
    block = 512
    steps = pl.cdiv(vocab, block)
    padded = steps * block
    full = lambda *shape: pl.BlockSpec(shape, lambda i, s: (0,) * len(shape))
    anywhere = pl.BlockSpec(memory_space=pl.ANY)
    smem = pl.BlockSpec(memory_space=pltpu.SMEM)
    count = sum(len(p[0]) for p in places)
    logits, note, whole, gram = pl.pallas_call(
        functools.partial(logits_kernel, places, vocab, steps),
        grid_spec=pltpu.PrefetchScalarGridSpec(
            num_scalar_prefetch=1,
            grid=(steps,),
            in_specs=[full(8, tokens)]
            + [anywhere] * len(pieces)
            + [pl.BlockSpec((block, model), lambda i, s: (i, 0))],
            out_specs=[
                pl.BlockSpec((block, tokens), lambda i, s: (i, 0)),
                full(devices, 8, tokens),
                full(tokens, model),
                full(tokens, tokens),
            ],
            scratch_shapes=[
                pltpu.VMEM((8, tokens), f32),
                pltpu.VMEM((8, tokens), f32),
                pltpu.SemaphoreType.DMA((count,)),
            ],
        ),
        out_shape=[
            jax.ShapeDtypeStruct((padded, tokens), f32),
            jax.ShapeDtypeStruct((devices, 8, tokens), f32),
            jax.ShapeDtypeStruct((tokens, model), bf16),
            jax.ShapeDtypeStruct((tokens, tokens), f32),
        ],
        cost_estimate=cost(2 * tokens * model * vocab, 2 * model * vocab),
        name="logits",
    )(at, own, *pieces, table)

    notes = lax.all_to_all(note, both, 0, 0)

    tall = divisor(width, 512)
    inner = width // tall
    scale = loss_scale.reshape(1, 1)

    def block_rows(flip):
        def index(i, s):
            dx = i // inner
            group = (s[2] ^ dx) * 2 + (s[3] ^ flip)
            return (0, group * inner + i % inner)

        return pl.BlockSpec((vocab, tall), index)

    parts = pl.BlockSpec((1, tokens, tall), lambda i, s: (i // inner, 0, i % inner))
    sent, grad, turned, sums = pl.pallas_call(
        functools.partial(gradient_kernel, vocab, block),
        grid_spec=pltpu.PrefetchScalarGridSpec(
            num_scalar_prefetch=1,
            grid=(2 * inner,),
            in_specs=[
                full(devices, 8, tokens),
                smem,
                full(padded, tokens),
                full(tokens, tokens),
                block_rows(1),
            ],
            out_specs=[parts, full(padded, tokens), full(tokens, padded), full(8, 128)],
        ),
        out_shape=[
            jax.ShapeDtypeStruct((2, tokens, width), bf16),
            jax.ShapeDtypeStruct((padded, tokens), bf16),
            jax.ShapeDtypeStruct((tokens, padded), bf16),
            jax.ShapeDtypeStruct((8, 128), f32),
        ],
        cost_estimate=cost(tokens * model * vocab, model * vocab),
        name="gradient",
    )(at, notes, scale, logits, gram, table)
    came = go(sent, dz=0, dy=0, dx=0, dc=1)
    twin = go(sums, dz=0, dy=0, dx=0, dc=1)
    kept = pl.pallas_call(
        functools.partial(product_kernel, vocab),
        grid_spec=pltpu.PrefetchScalarGridSpec(
            num_scalar_prefetch=1,
            grid=(2 * inner,),
            in_specs=[full(tokens, padded), block_rows(0)],
            out_specs=parts,
        ),
        out_shape=jax.ShapeDtypeStruct((2, tokens, width), f32),
        cost_estimate=cost(tokens * model * vocab, model * vocab),
        name="product",
    )(at, turned, table)

    pair = sums[0, :2] + twin[0, :2]
    total = (kept + came.astype(f32)).reshape(2, levels, 2, rows, width)
    near = lambda dx, dy: lax.dynamic_index_in_dim(total[dx], y ^ dy, axis=1, keepdims=False)
    far = near(1, 1)
    shape = (-1, rows, width)
    open_up = lambda message: (
        message[:-8].reshape(shape).astype(f32),
        decoded(message[-8], 2),
    )
    from_x, pair_x = open_up(go(packed(far[:half], pair, width), dz=0, dy=0, dx=1, dc=0))
    from_y, pair_y = open_up(go(packed(far[half:], pair, width), dz=0, dy=1, dx=0, dc=0))
    for_x, for_y = near(1, 0), near(0, 1)
    for_x = jnp.concatenate([for_x[:half], for_x[half:] + from_y])
    for_y = jnp.concatenate([for_y[:half] + from_x, for_y[half:]])
    got_x, cross = open_up(go(packed(for_x, pair + pair_y, width), dz=0, dy=0, dx=1, dc=0))
    got_y = go(for_y.astype(bf16), dz=0, dy=1, dx=0, dc=0).astype(f32)
    layer = near(0, 0) + got_x + got_y
    quad = pair + pair_y + cross
    pick = lambda d: lax.dynamic_index_in_dim(layer, z ^ d, axis=0, keepdims=False)
    result, both_sums = pick(0), quad
    for d in range(1, levels):
        message, value = open_up(go(packed(pick(d), quad, width), dz=d, dy=0, dx=0, dc=0))
        result += message[0]
        both_sums += value
    grad_hidden = result.astype(bf16)

    squares, hits = both_sums[0], both_sums[1]
    loss = (sums[0, 2] - hits) / sums[0, 3]
    grad_norm = jnp.sqrt(jnp.maximum(squares, 0.0)) / loss_scale
    rate = (clip_limit / jnp.maximum(grad_norm, clip_limit)).reshape(1, 1)
    grad_weight = pl.pallas_call(
        functools.partial(outer_kernel, block),
        grid=(steps,),
        in_specs=[
            smem,
            pl.BlockSpec((tokens, model), lambda i: (0, 0)),
            pl.BlockSpec((block, tokens), lambda i: (i, 0)),
        ],
        out_specs=pl.BlockSpec((block, model), lambda i: (i, 0)),
        out_shape=jax.ShapeDtypeStruct((vocab, model), bf16),
        cost_estimate=cost(2 * tokens * model * vocab, 2 * model * vocab),
        name="outer",
    )(rate, whole, grad).T
    return (loss, grad_hidden, grad_weight)


def solution(mesh):
    placed = (
        P("context", "tensor"),
        P(None, both),
        P("context"),
        P("context"),
        P(),
    )
    return jax.shard_map(
        functools.partial(shards, mesh.shape["context"], mesh.shape["tensor"]),
        mesh=mesh,
        in_specs=placed,
        out_specs=(P(), P("context", "tensor"), P(None, both)),
        check_vma=False,
    )
```

time: 316 us -> 143 us (0.45)
  blocking collectives: 126 us -> 0 us
  Pallas kernels: 0 us -> 62.3 us
  matrix products: 61.3 us -> 0 us
  other arithmetic: 36.7 us -> 5.65 us
  waiting for transfers between devices: 66 us -> 39.7 us
  starting transfers between devices: 0.3 us -> 24.5 us
  between operations: 18.4 us -> 5.47 us
    all_gather x7 -> x0, blocking collectives: 76.7 us -> none  [the longest x6 67.9 us: joined(): pieces = jax.tree.map(lambda part: lax.all_gather(part, axis), value)]
    pallas_call x0 -> x4, Pallas kernels: none -> 62.3 us  [the longest x1 22.1 us: shards(): pl.pallas_call(functools.partial(logits_kernel, places, vocab, steps), gr...]
    dot_general x3 -> x0, matrix products: 61.3 us -> none  [the longest x1 27.5 us: shards(): lax.dot_general(all_rows, grad_logits, (((0,), (0,)), ((), ())), preferre...]
    psum x1 -> x0, blocking collectives: 37.6 us -> none  [shards(): squares = lax.psum(jnp.sum(raw_grad * raw_grad), ('context', 'tensor'))]
    all_gather x1 -> x0, waiting for transfers between devices: 33.6 us -> none  [shards(): lax.all_gather(rows, 'context', axis=0, tiled=True)]
    convert_element_type x2 -> x6, other arithmetic: 34 us -> 0.67 us  [the longest x1 0.66 us: shards(): grad_hidden = result.astype(bf16)]
    reduce_scatter x2 -> x0, waiting for transfers between devices: 32.4 us -> none  [the longest x1 32.3 us: shards(): lax.psum_scatter(feature_part, 'context', scatter_dimension=0, tiled=True)]
    ppermute x0 -> x21, waiting for transfers between devices: none -> 29.8 us  [hop(): return lax.ppermute(value, both, pairs)]
  transfers between devices with their start and end apart: 3 -> 22, of which waited for: 2 -> 11; matrix products, arithmetic and copies ran while one was open for 20% -> 3% of each run, Pallas kernels for 0% -> 8%
where the time goes in v1:
time: 143 us
  Pallas kernels  62.3 us (44%)
  waiting for transfers between devices  39.7 us (28%)
  starting transfers between devices  24.5 us (17%)
  other arithmetic  5.65 us (4%)
  between operations  5.47 us (4%)
  local copies, waits for them, and re-layouts  5.01 us (4%)
    ppermute x21, waiting for transfers between devices, hop(): return lax.ppermute(value, both, pairs)  29.8 us
    pallas_call x1, Pallas kernels, shards(): pl.pallas_call(functools.partial(logits_kernel, places, vocab, steps), gr...  22.1 us
    ppermute x21, starting transfers between devices, hop(): return lax.ppermute(value, both, pairs)  21.5 us
    pallas_call x1, Pallas kernels, shards(): pl.pallas_call(functools.partial(outer_kernel, block), grid=(steps,), in_...  15.9 us
    pallas_call x1, Pallas kernels, shards(): pl.pallas_call(functools.partial(gradient_kernel, vocab, block), grid_spe...  13.4 us
    pallas_call x1, Pallas kernels, shards(): pl.pallas_call(functools.partial(product_kernel, vocab), grid_spec=pltpu....  10.9 us
    all_to_all x1, waiting for transfers between devices, shards(): notes = lax.all_to_all(note, both, 0, 0)  9.93 us
    all_to_all x1, starting transfers between devices, shards(): notes = lax.all_to_all(note, both, 0, 0)  3.04 us
  transfers between devices with their start and end apart: 22, of which 11 were waited for; matrix products, arithmetic and copies ran while one was open for 3% of the time, Pallas kernels for 8%

profile of v1, /device:TPU:0, one launch (start us, length us, event | category | flops | bytes accessed | tf_op | source)
XLA Modules:
  0.0 142.7 jit_solution(833190408780945338)
XLA Ops:
  0.6 3.1 %collective-permute-start = (bf16[32,1024]{1,0:T(8,128)(2,1)}, bf16[32,1024]{1,0:T(8,128)(2,1)S(1)}, u32[]{:S(2)}, u32[]{:S(2)}) collective-permute-start(bf16[32,1024]{1,0:T(8,128)(2,1)} %param.5), channel_id=1, source_target_pairs={{0,8},{1,9},{2,10},{3,11},{4,12},{5,13},{6,14},{7,15},{8,0},{9,1},... | collective-permute-start | bytes 196616 | tf_op jit(solution)/shard_map/ppermute | solution.py:34
  3.7 2.5 %collective-permute-start.2 = (bf16[32,1024]{1,0:T(8,128)(2,1)}, bf16[32,1024]{1,0:T(8,128)(2,1)S(1)}, u32[]{:S(2)}, u32[]{:S(2)}) collective-permute-start(bf16[32,1024]{1,0:T(8,128)(2,1)} %param.5), channel_id=1, source_target_pairs={{0,24},{1,25},{2,26},{3,27},{4,28},{5,29},{6,30},{7,31},{8,16},{9,... | collective-permute-start | bytes 196616 | tf_op jit(solution)/shard_map/ppermute | solution.py:34
  6.2 0.1 collective-permute-start.1
  6.3 0.0 collective-permute-done
  6.3 4.5 %collective-permute-done.2 = bf16[32,1024]{1,0:T(8,128)(2,1)S(1)} collective-permute-done((bf16[32,1024]{1,0:T(8,128)(2,1)}, bf16[32,1024]{1,0:T(8,128)(2,1)S(1)}, u32[]{:S(2)}, u32[]{:S(2)}) %collective-permute-start.2) | collective-permute-done | bytes 65568 | tf_op jit(solution)/shard_map/ppermute | solution.py:34
  10.8 2.1 %collective-permute-done.1 = bf16[32,1024]{1,0:T(8,128)(2,1)S(1)} collective-permute-done((bf16[32,1024]{1,0:T(8,128)(2,1)}, bf16[32,1024]{1,0:T(8,128)(2,1)S(1)}, u32[]{:S(2)}, u32[]{:S(2)}) %collective-permute-start.1) | collective-permute-done | bytes 65568 | tf_op jit(solution)/shard_map/ppermute | solution.py:34
  12.9 0.9 pad_maximum_fusion.1.refs_0_
  13.8 1.6 %collective-permute-start.4 = (bf16[4,32,1024]{2,1,0:T(8,128)(2,1)S(1)}, bf16[4,32,1024]{2,1,0:T(8,128)(2,1)S(1)}, u32[]{:S(2)}, u32[]{:S(2)}) collective-permute-start(bf16[4,32,1024]{2,1,0:T(8,128)(2,1)S(1)} %pad_maximum_fusion.1.refs_0_), channel_id=1, source_target_pairs={{0,4},{1,5},{2,6},{3,7},{4,0},{5,1},{6,2},{7,3},{8,12},{9,13},{10,... | collective-permute-start | bytes 786440 | tf_op jit(solution)/shard_map/ppermute | solution.py:34
  15.4 1.5 %collective-permute-start.3 = (bf16[4,32,1024]{2,1,0:T(8,128)(2,1)S(1)}, bf16[4,32,1024]{2,1,0:T(8,128)(2,1)S(1)}, u32[]{:S(2)}, u32[]{:S(2)}) collective-permute-start(bf16[4,32,1024]{2,1,0:T(8,128)(2,1)S(1)} %pad_maximum_fusion.1.refs_0_), channel_id=1, source_target_pairs={{0,2},{1,3},{2,0},{3,1},{4,6},{5,7},{6,4},{7,5},{8,10},{9,11},{10,... | collective-permute-start | bytes 786440 | tf_op jit(solution)/shard_map/ppermute | solution.py:34
  16.9 5.1 %collective-permute-done.4.refs_2_ = bf16[4,32,1024]{2,1,0:T(8,128)(2,1)S(1)} collective-permute-done((bf16[4,32,1024]{2,1,0:T(8,128)(2,1)S(1)}, bf16[4,32,1024]{2,1,0:T(8,128)(2,1)S(1)}, u32[]{:S(2)}, u32[]{:S(2)}) %collective-permute-start.4) | collective-permute-done | bytes 262176 | tf_op jit(solution)/shard_map/ppermute | solution.py:34
  22.0 1.6 %collective-permute-start.5 = (bf16[2,32,1024]{2,1,0:T(8,128)(2,1)S(1)}, bf16[2,32,1024]{2,1,0:T(8,128)(2,1)S(1)}, u32[]{:S(2)}, u32[]{:S(2)}) collective-permute-start(bf16[2,32,1024]{2,1,0:T(8,128)(2,1)S(1)} %slice.224), channel_id=1, source_target_pairs={{0,2},{1,3},{2,0},{3,1},{4,6},{5,7},{6,4},{7,5},{8,10},{9,11},{10,... | collective-permute-start | bytes 393224 | tf_op jit(solution)/shard_map/ppermute | solution.py:34
  23.6 0.0 collective-permute-start.9
  23.6 0.0 collective-permute-done.3.refs_1_
  23.6 0.6 collective-permute-start.8
  24.2 1.5 %collective-permute-start.6 = (bf16[2,32,1024]{2,1,0:T(8,128)(2,1)S(1)}, bf16[2,32,1024]{2,1,0:T(8,128)(2,1)S(1)}, u32[]{:S(2)}, u32[]{:S(2)}) collective-permute-start(bf16[2,32,1024]{2,1,0:T(8,128)(2,1)S(1)} %slice.225), channel_id=1, source_target_pairs={{0,4},{1,5},{2,6},{3,7},{4,0},{5,1},{6,2},{7,3},{8,12},{9,13},{10,... | collective-permute-start | bytes 393224 | tf_op jit(solution)/shard_map/ppermute | solution.py:34
  25.7 1.4 collective-permute-done.5.refs_3_
  27.1 0.0 collective-permute-start.10
  27.1 2.6 %collective-permute-done.6.refs_4_ = bf16[2,32,1024]{2,1,0:T(8,128)(2,1)S(1)} collective-permute-done((bf16[2,32,1024]{2,1,0:T(8,128)(2,1)S(1)}, bf16[2,32,1024]{2,1,0:T(8,128)(2,1)S(1)}, u32[]{:S(2)}, u32[]{:S(2)}) %collective-permute-start.6) | collective-permute-done | bytes 131104 | tf_op jit(solution)/shard_map/ppermute | solution.py:34
  29.7 0.0 collective-permute-start.11
  29.7 0.7 fusion.28
  30.4 0.4 dynamic_update_slice.3.own_ref
  30.8 0.0 copy-start.11
  30.8 0.6 stack.47.at_ref
  31.4 0.0 collective-permute-done.8.refs_6_
  31.6 0.6 copy-done.4
  32.1 0.1 copy-done.5
  32.2 0.1 copy-done.6
  32.3 0.0 copy-done.9
  32.3 0.0 copy-done.10
  32.4 22.1 %logits.1 = (f32[4096,256]{1,0:T(8,128)}, f32[32,8,256]{2,1,0:T(8,128)}, bf16[256,4096]{1,0:T(8,128)(2,1)}, f32[256,256]{1,0:T(8,128)}) custom-call(s32[5]{0:T(128)} %stack.47.at_ref, f32[8,256]{1,0:T(8,128)} %copy-done.11, bf16[4,32,1024]{2,1,0:T(8,128)(2,1)} %copy-done, bf16[4,32,1024]{2,1,0:T(8,128)(2,1)} %copy-done.3, bf16[4,32,1024]{2,1,0:T(8,128)(2,1)} %copy-done.2, ...), custom_call_target="tpu_custom_call" | custom-call | flops 8405385216 | bytes 32833536 | tf_op jit(solution)/shard_map/logits/pallas_call | solution.py:229
  54.5 3.0 %all-to-all-start = ((f32[32,8,256]{2,1,0:T(8,128)}), f32[32,8,256]{2,1,0:T(8,128)S(1)}, u32[]{:S(2)}, u32[]{:S(2)}) async-start(f32[32,8,256]{2,1,0:T(8,128)} %get-tuple-element.11), calls=%async_computation | async-start | bytes 524288 | tf_op jit(solution)/shard_map/all_to_all | solution.py:259
  58.2 9.9 %all-to-all-done.notes_ref = f32[32,8,256]{2,1,0:T(8,128)S(1)} async-done(((f32[32,8,256]{2,1,0:T(8,128)}), f32[32,8,256]{2,1,0:T(8,128)S(1)}, u32[]{:S(2)}, u32[]{:S(2)}) %all-to-all-start) | async-done | bytes 262176 | tf_op jit(solution)/shard_map/all_to_all | solution.py:259
  68.1 0.7 copy-done.1
  68.8 13.4 %gradient.1 = (bf16[2,256,1024]{2,1,0:T(8,128)(2,1)}, bf16[4096,256]{1,0:T(8,128)(2,1)}, bf16[256,4096]{1,0:T(8,128)(2,1)}, f32[8,128]{1,0:T(8,128)}) custom-call(s32[5]{0:T(128)} %stack.47.at_ref, f32[32,8,256]{2,1,0:T(8,128)} %copy-done.1, f32[1,1]{1,0:T(1,128)} %bitcast.91.scale_ref, f32[4096,256]{1,0:T(8,128)} %get-tuple-element.12.logits_ref, ...), custom_call_target="tpu_custom_call" | custom-call | flops 4202692608 | bytes 16416768 | tf_op jit(solution)/shard_map/gradient/pallas_call | solution.py:274
  82.2 0.0 collective-permute-start.13
  82.3 0.5 collective-permute-start.12
  82.7 10.9 %product.1 = f32[2,256,1024]{2,1,0:T(8,128)} custom-call(s32[5]{0:T(128)} %stack.47.at_ref, bf16[256,4096]{1,0:T(8,128)(2,1)} %get-tuple-element.15.turned_ref, bf16[4008,4096]{1,0:T(8,128)(2,1)} %bitcast.94), custom_call_target="tpu_custom_call" | custom-call | flops 4202692608 | bytes 16416768 | tf_op jit(solution)/shard_map/product/pallas_call | solution.py:299
  93.6 0.7 reduce-precision_convert_fusion.5
  94.3 0.1 fusion.23
  94.4 1.9 %convert_add_fusion = f32[2,256,1024]{2,1,0:T(8,128)S(1)} fusion(f32[2,256,1024]{2,1,0:T(8,128)} %product.1, bf16[2,256,1024]{2,1,0:T(8,128)(2,1)S(1)} %collective-permute-done.13), kind=kLoop, calls=%fused_computation | loop fusion | flops 1048576 | bytes 5242880 | tf_op jit(solution)/shard_map/add | solution.py:313
  96.3 0.2 fusion.35
  96.6 0.1 dynamic-slice_bitcast_fusion.1
  96.8 0.5 collective-permute-start.16
  97.3 1.3 collective-permute-start.14
  98.6 4.5 %collective-permute-done.14 = bf16[72,1024]{1,0:T(8,128)(2,1)S(1)} collective-permute-done((bf16[72,1024]{1,0:T(8,128)(2,1)S(1)}, bf16[72,1024]{1,0:T(8,128)(2,1)S(1)}, u32[]{:S(2)}, u32[]{:S(2)}) %collective-permute-start.14) | collective-permute-done | bytes 147488 | tf_op jit(solution)/shard_map/ppermute | solution.py:34
  103.1 0.1 reduce-precision_convert_fusion.3
  103.3 0.1 fusion.25
  103.4 1.4 collective-permute-start.15
  104.9 1.0 collective-permute-start.17
  105.9 5.5 %collective-permute-done.15 = bf16[136,1024]{1,0:T(8,128)(2,1)S(1)} collective-permute-done((bf16[136,1024]{1,0:T(8,128)(2,1)S(1)}, bf16[136,1024]{1,0:T(8,128)(2,1)S(1)}, u32[]{:S(2)}, u32[]{:S(2)}) %collective-permute-start.15) | collective-permute-done | bytes 278560 | tf_op jit(solution)/shard_map/ppermute | solution.py:34
  111.3 0.1 reduce-precision_convert_fusion.1
  111.4 0.1 fusion.27
  111.5 0.4 collective-permute-done.17
  111.9 0.1 fusion
  112.1 1.0 collective-permute-start.18
  113.1 1.3 fusion.37
  114.4 1.0 collective-permute-start.19
  115.4 2.5 %collective-permute-start.20 = (bf16[40,1024]{1,0:T(8,128)(2,1)S(1)}, bf16[40,1024]{1,0:T(8,128)(2,1)S(1)}, u32[]{:S(2)}, u32[]{:S(2)}) collective-permute-start(bf16[40,1024]{1,0:T(8,128)(2,1)S(1)} %get-tuple-element.36), channel_id=1, source_target_pairs={{0,24},{1,25},{2,26},{3,27},{4,28},{5,29},{6,30},{7,31},{8,16},{9,... | collective-permute-start | bytes 245768 | tf_op jit(solution)/shard_map/ppermute | solution.py:34
  117.9 2.8 %collective-permute-done.19 = bf16[40,1024]{1,0:T(8,128)(2,1)S(1)} collective-permute-done((bf16[40,1024]{1,0:T(8,128)(2,1)S(1)}, bf16[40,1024]{1,0:T(8,128)(2,1)S(1)}, u32[]{:S(2)}, u32[]{:S(2)}) %collective-permute-start.19) | collective-permute-done | bytes 81952 | tf_op jit(solution)/shard_map/ppermute | solution.py:34
  120.7 0.9 collective-permute-done.20
  121.6 0.1 bitcast_add_fusion.1
  121.7 0.6 fusion.38
  125.0 15.9 %outer.1 = bf16[4008,4096]{1,0:T(8,128)(2,1)} custom-call(f32[1,1]{1,0:T(1,128)} %bitcast.41.rate_ref, bf16[256,4096]{1,0:T(8,128)(2,1)} %get-tuple-element.17.hidden_ref, bf16[4096,256]{1,0:T(8,128)(2,1)} %get-tuple-element.18.grad_ref), custom_call_target="tpu_custom_call" | custom-call | flops 8405385216 | bytes 32833536 | tf_op jit(solution)/shard_map/outer/pallas_call | solution.py:342
  140.9 0.7 fusion.9
  (55 shorter events, 0.5 us)
Async XLA Ops:
  0.6 5.7 %collective-permute-start = (bf16[32,1024]{1,0:T(8,128)(2,1)}, bf16[32,1024]{1,0:T(8,128)(2,1)S(1)}, u32[]{:S(2)}, u32[]{:S(2)}) collective-permute-start(bf16[32,1024]{1,0:T(8,128)(2,1)} %param.5), channel_id=1, source_target_pairs={{0,8},{1,9},{2,10},{3,11},{4,12},{5,13},{6,14},{7,15},{8,0},{9,1},... | collective-permute-start | bytes 196616 | tf_op jit(solution)/shard_map/ppermute | solution.py:34
  3.7 7.1 %collective-permute-start.2 = (bf16[32,1024]{1,0:T(8,128)(2,1)}, bf16[32,1024]{1,0:T(8,128)(2,1)S(1)}, u32[]{:S(2)}, u32[]{:S(2)}) collective-permute-start(bf16[32,1024]{1,0:T(8,128)(2,1)} %param.5), channel_id=1, source_target_pairs={{0,24},{1,25},{2,26},{3,27},{4,28},{5,29},{6,30},{7,31},{8,16},{9,... | collective-permute-start | bytes 196616 | tf_op jit(solution)/shard_map/ppermute | solution.py:34
  6.2 6.7 %collective-permute-start.1 = (bf16[32,1024]{1,0:T(8,128)(2,1)}, bf16[32,1024]{1,0:T(8,128)(2,1)S(1)}, u32[]{:S(2)}, u32[]{:S(2)}) collective-permute-start(bf16[32,1024]{1,0:T(8,128)(2,1)} %param.5), channel_id=1, source_target_pairs={{0,16},{1,17},{2,18},{3,19},{4,20},{5,21},{6,22},{7,23},{8,24},{9,... | collective-permute-start | bytes 196616 | tf_op jit(solution)/shard_map/ppermute | solution.py:34
  13.8 17.7 %copy-start = (bf16[4,32,1024]{2,1,0:T(8,128)(2,1)}, bf16[4,32,1024]{2,1,0:T(8,128)(2,1)S(1)}, u32[]{:S(2)}) copy-start(bf16[4,32,1024]{2,1,0:T(8,128)(2,1)S(1)} %pad_maximum_fusion.1.refs_0_) | copy-start | bytes 786436
  13.8 8.2 %collective-permute-start.4 = (bf16[4,32,1024]{2,1,0:T(8,128)(2,1)S(1)}, bf16[4,32,1024]{2,1,0:T(8,128)(2,1)S(1)}, u32[]{:S(2)}, u32[]{:S(2)}) collective-permute-start(bf16[4,32,1024]{2,1,0:T(8,128)(2,1)S(1)} %pad_maximum_fusion.1.refs_0_), channel_id=1, source_target_pairs={{0,4},{1,5},{2,6},{3,7},{4,0},{5,1},{6,2},{7,3},{8,12},{9,13},{10,... | collective-permute-start | bytes 786440 | tf_op jit(solution)/shard_map/ppermute | solution.py:34
  15.4 8.2 %collective-permute-start.3 = (bf16[4,32,1024]{2,1,0:T(8,128)(2,1)S(1)}, bf16[4,32,1024]{2,1,0:T(8,128)(2,1)S(1)}, u32[]{:S(2)}, u32[]{:S(2)}) collective-permute-start(bf16[4,32,1024]{2,1,0:T(8,128)(2,1)S(1)} %pad_maximum_fusion.1.refs_0_), channel_id=1, source_target_pairs={{0,2},{1,3},{2,0},{3,1},{4,6},{5,7},{6,4},{7,5},{8,10},{9,11},{10,... | collective-permute-start | bytes 786440 | tf_op jit(solution)/shard_map/ppermute | solution.py:34
  16.9 14.6 %collective-permute-start.7 = (bf16[4,32,1024]{2,1,0:T(8,128)(2,1)S(1)}, bf16[4,32,1024]{2,1,0:T(8,128)(2,1)S(1)}, u32[]{:S(2)}, u32[]{:S(2)}) collective-permute-start(bf16[4,32,1024]{2,1,0:T(8,128)(2,1)S(1)} %pad_maximum_fusion.1.refs_0_), channel_id=1, source_target_pairs={{0,1},{1,0},{2,3},{3,2},{4,5},{5,4},{6,7},{7,6},{8,9},{9,8},{10,11... | collective-permute-start | bytes 786440 | tf_op jit(solution)/shard_map/ppermute | solution.py:34
  22.0 9.5 %copy-start.2 = (bf16[4,32,1024]{2,1,0:T(8,128)(2,1)}, bf16[4,32,1024]{2,1,0:T(8,128)(2,1)S(1)}, u32[]{:S(2)}) copy-start(bf16[4,32,1024]{2,1,0:T(8,128)(2,1)S(1)} %collective-permute-done.4.refs_2_) | copy-start | bytes 786436
  22.0 5.0 %collective-permute-start.5 = (bf16[2,32,1024]{2,1,0:T(8,128)(2,1)S(1)}, bf16[2,32,1024]{2,1,0:T(8,128)(2,1)S(1)}, u32[]{:S(2)}, u32[]{:S(2)}) collective-permute-start(bf16[2,32,1024]{2,1,0:T(8,128)(2,1)S(1)} %slice.224), channel_id=1, source_target_pairs={{0,2},{1,3},{2,0},{3,1},{4,6},{5,7},{6,4},{7,5},{8,10},{9,11},{10,... | collective-permute-start | bytes 393224 | tf_op jit(solution)/shard_map/ppermute | solution.py:34
  23.6 7.8 %collective-permute-start.9 = (bf16[4,32,1024]{2,1,0:T(8,128)(2,1)S(1)}, bf16[4,32,1024]{2,1,0:T(8,128)(2,1)S(1)}, u32[]{:S(2)}, u32[]{:S(2)}) collective-permute-start(bf16[4,32,1024]{2,1,0:T(8,128)(2,1)S(1)} %collective-permute-done.4.refs_2_), channel_id=1, source_target_pairs={{0,1},{1,0},{2,3},{3,2},{4,5},{5,4},{6,7},{7,6},{8,9},{9,8},{10,11... | collective-permute-start | bytes 786440 | tf_op jit(solution)/shard_map/ppermute | solution.py:34
  23.6 7.9 %copy-start.3 = (bf16[4,32,1024]{2,1,0:T(8,128)(2,1)}, bf16[4,32,1024]{2,1,0:T(8,128)(2,1)S(1)}, u32[]{:S(2)}) copy-start(bf16[4,32,1024]{2,1,0:T(8,128)(2,1)S(1)} %collective-permute-done.3.refs_1_) | copy-start | bytes 786436
  23.6 7.8 %collective-permute-start.8 = (bf16[4,32,1024]{2,1,0:T(8,128)(2,1)S(1)}, bf16[4,32,1024]{2,1,0:T(8,128)(2,1)S(1)}, u32[]{:S(2)}, u32[]{:S(2)}) collective-permute-start(bf16[4,32,1024]{2,1,0:T(8,128)(2,1)S(1)} %collective-permute-done.3.refs_1_), channel_id=1, source_target_pairs={{0,1},{1,0},{2,3},{3,2},{4,5},{5,4},{6,7},{7,6},{8,9},{9,8},{10,11... | collective-permute-start | bytes 786440 | tf_op jit(solution)/shard_map/ppermute | solution.py:34
  24.2 5.5 %collective-permute-start.6 = (bf16[2,32,1024]{2,1,0:T(8,128)(2,1)S(1)}, bf16[2,32,1024]{2,1,0:T(8,128)(2,1)S(1)}, u32[]{:S(2)}, u32[]{:S(2)}) collective-permute-start(bf16[2,32,1024]{2,1,0:T(8,128)(2,1)S(1)} %slice.225), channel_id=1, source_target_pairs={{0,4},{1,5},{2,6},{3,7},{4,0},{5,1},{6,2},{7,3},{8,12},{9,13},{10,... | collective-permute-start | bytes 393224 | tf_op jit(solution)/shard_map/ppermute | solution.py:34
  27.1 4.5 %copy-start.7 = (bf16[2,32,1024]{2,1,0:T(8,128)(2,1)}, bf16[2,32,1024]{2,1,0:T(8,128)(2,1)S(1)}, u32[]{:S(2)}) copy-start(bf16[2,32,1024]{2,1,0:T(8,128)(2,1)S(1)} %collective-permute-done.5.refs_3_) | copy-start | bytes 393220
  27.1 4.4 %collective-permute-start.10 = (bf16[2,32,1024]{2,1,0:T(8,128)(2,1)S(1)}, bf16[2,32,1024]{2,1,0:T(8,128)(2,1)S(1)}, u32[]{:S(2)}, u32[]{:S(2)}) collective-permute-start(bf16[2,32,1024]{2,1,0:T(8,128)(2,1)S(1)} %collective-permute-done.5.refs_3_), channel_id=1, source_target_pairs={{0,1},{1,0},{2,3},{3,2},{4,5},{5,4},{6,7},{7,6},{8,9},{9,8},{10,11... | collective-permute-start | bytes 393224 | tf_op jit(solution)/shard_map/ppermute | solution.py:34
  29.7 1.9 %copy-start.8 = (bf16[2,32,1024]{2,1,0:T(8,128)(2,1)}, bf16[2,32,1024]{2,1,0:T(8,128)(2,1)S(1)}, u32[]{:S(2)}) copy-start(bf16[2,32,1024]{2,1,0:T(8,128)(2,1)S(1)} %collective-permute-done.6.refs_4_) | copy-start | bytes 393220
  29.7 1.8 %collective-permute-start.11 = (bf16[2,32,1024]{2,1,0:T(8,128)(2,1)S(1)}, bf16[2,32,1024]{2,1,0:T(8,128)(2,1)S(1)}, u32[]{:S(2)}, u32[]{:S(2)}) collective-permute-start(bf16[2,32,1024]{2,1,0:T(8,128)(2,1)S(1)} %collective-permute-done.6.refs_4_), channel_id=1, source_target_pairs={{0,1},{1,0},{2,3},{3,2},{4,5},{5,4},{6,7},{7,6},{8,9},{9,8},{10,11... | collective-permute-start | bytes 393224 | tf_op jit(solution)/shard_map/ppermute | solution.py:34
  30.8 0.8 copy-start.11
  31.4 0.7 copy-start.4
  31.4 0.8 copy-start.5
  31.4 0.9 copy-start.6
  31.5 0.9 copy-start.9
  31.5 0.9 copy-start.10
  54.5 13.6 %all-to-all-start = ((f32[32,8,256]{2,1,0:T(8,128)}), f32[32,8,256]{2,1,0:T(8,128)S(1)}, u32[]{:S(2)}, u32[]{:S(2)}) async-start(f32[32,8,256]{2,1,0:T(8,128)} %get-tuple-element.11), calls=%async_computation | async-start | bytes 524288 | tf_op jit(solution)/shard_map/all_to_all | solution.py:259
  68.1 0.7 copy-start.1
  82.2 12.2 %collective-permute-start.13 = (bf16[2,256,1024]{2,1,0:T(8,128)(2,1)}, bf16[2,256,1024]{2,1,0:T(8,128)(2,1)S(1)}, u32[]{:S(2)}, u32[]{:S(2)}) collective-permute-start(bf16[2,256,1024]{2,1,0:T(8,128)(2,1)} %get-tuple-element.16), channel_id=1, source_target_pairs={{0,1},{1,0},{2,3},{3,2},{4,5},{5,4},{6,7},{7,6},{8,9},{9,8},{10,11... | collective-permute-start | bytes 3145736 | tf_op jit(solution)/shard_map/ppermute | solution.py:34
  82.3 11.4 %collective-permute-start.12 = (f32[8,128]{1,0:T(8,128)}, f32[8,128]{1,0:T(8,128)S(1)}, u32[]{:S(2)}, u32[]{:S(2)}) collective-permute-start(f32[8,128]{1,0:T(8,128)} %get-tuple-element.14), channel_id=1, source_target_pairs={{0,1},{1,0},{2,3},{3,2},{4,5},{5,4},{6,7},{7,6},{8,9},{9,8},{10,11... | collective-permute-start | bytes 12296 | tf_op jit(solution)/shard_map/ppermute | solution.py:34
  96.8 8.0 %collective-permute-start.16 = (bf16[72,1024]{1,0:T(8,128)(2,1)S(1)}, bf16[72,1024]{1,0:T(8,128)(2,1)S(1)}, u32[]{:S(2)}, u32[]{:S(2)}) collective-permute-start(bf16[72,1024]{1,0:T(8,128)(2,1)S(1)} %get-tuple-element.37), channel_id=1, source_target_pairs={{0,2},{1,3},{2,0},{3,1},{4,6},{5,7},{6,4},{7,5},{8,10},{9,11},{10,... | collective-permute-start | bytes 442376 | tf_op jit(solution)/shard_map/ppermute | solution.py:34
  97.3 5.9 %collective-permute-start.14 = (bf16[72,1024]{1,0:T(8,128)(2,1)S(1)}, bf16[72,1024]{1,0:T(8,128)(2,1)S(1)}, u32[]{:S(2)}, u32[]{:S(2)}) collective-permute-start(bf16[72,1024]{1,0:T(8,128)(2,1)S(1)} %get-tuple-element.38), channel_id=1, source_target_pairs={{0,4},{1,5},{2,6},{3,7},{4,0},{5,1},{6,2},{7,3},{8,12},{9,13},{10,... | collective-permute-start | bytes 442376 | tf_op jit(solution)/shard_map/ppermute | solution.py:34
  103.4 7.9 %collective-permute-start.15 = (bf16[136,1024]{1,0:T(8,128)(2,1)S(1)}, bf16[136,1024]{1,0:T(8,128)(2,1)S(1)}, u32[]{:S(2)}, u32[]{:S(2)}) collective-permute-start(bf16[136,1024]{1,0:T(8,128)(2,1)S(1)} %pad_maximum_fusion), channel_id=1, source_target_pairs={{0,2},{1,3},{2,0},{3,1},{4,6},{5,7},{6,4},{7,5},{8,10},{9,11},{10,... | collective-permute-start | bytes 835592 | tf_op jit(solution)/shard_map/ppermute | solution.py:34
  104.9 7.0 %collective-permute-start.17 = (bf16[4,32,1024]{2,1,0:T(8,128)(2,1)S(1)}, bf16[4,32,1024]{2,1,0:T(8,128)(2,1)S(1)}, u32[]{:S(2)}, u32[]{:S(2)}) collective-permute-start(bf16[4,32,1024]{2,1,0:T(8,128)(2,1)S(1)} %pad_maximum_fusion.3), channel_id=1, source_target_pairs={{0,4},{1,5},{2,6},{3,7},{4,0},{5,1},{6,2},{7,3},{8,12},{9,13},{10,... | collective-permute-start | bytes 786440 | tf_op jit(solution)/shard_map/ppermute | solution.py:34
  112.1 5.8 %collective-permute-start.18 = (bf16[40,1024]{1,0:T(8,128)(2,1)S(1)}, bf16[40,1024]{1,0:T(8,128)(2,1)S(1)}, u32[]{:S(2)}, u32[]{:S(2)}) collective-permute-start(bf16[40,1024]{1,0:T(8,128)(2,1)S(1)} %get-tuple-element.34), channel_id=1, source_target_pairs={{0,8},{1,9},{2,10},{3,11},{4,12},{5,13},{6,14},{7,15},{8,0},{9,1},... | collective-permute-start | bytes 245768 | tf_op jit(solution)/shard_map/ppermute | solution.py:34
  114.4 6.3 %collective-permute-start.19 = (bf16[40,1024]{1,0:T(8,128)(2,1)S(1)}, bf16[40,1024]{1,0:T(8,128)(2,1)S(1)}, u32[]{:S(2)}, u32[]{:S(2)}) collective-permute-start(bf16[40,1024]{1,0:T(8,128)(2,1)S(1)} %get-tuple-element.35), channel_id=1, source_target_pairs={{0,16},{1,17},{2,18},{3,19},{4,20},{5,21},{6,22},{7,23},{8,24},{9,... | collective-permute-start | bytes 245768 | tf_op jit(solution)/shard_map/ppermute | solution.py:34
  115.4 6.2 %collective-permute-start.20 = (bf16[40,1024]{1,0:T(8,128)(2,1)S(1)}, bf16[40,1024]{1,0:T(8,128)(2,1)S(1)}, u32[]{:S(2)}, u32[]{:S(2)}) collective-permute-start(bf16[40,1024]{1,0:T(8,128)(2,1)S(1)} %get-tuple-element.36), channel_id=1, source_target_pairs={{0,24},{1,25},{2,26},{3,27},{4,28},{5,29},{6,30},{7,31},{8,16},{9,... | collective-permute-start | bytes 245768 | tf_op jit(solution)/shard_map/ppermute | solution.py:34
